TPU v7x, 32 devices: a whole 2x2x4 slice. The times are simulated.
32 devices in a mesh: groups: 2 (over y), dp: 4 (over z), mp: 4 (over x, core).
Axes of the slice: x: 2, y: 2, z: 4, core: 2. Of those that a mesh axis runs over, the one named last changes fastest.
Arguments:
- hidden: bfloat16 [8, 8192], P(('groups', 'mp'), 'dp'), parts along dimension 0, may hold values from -530 to 530
- attention_gain: float32 [8192], P('dp'), may hold values from 0.25 to 1.75
- query_weight: bfloat16 [8192, 8192], P('dp', 'mp'), may hold values from -0.0625 to 0.0625
- key_projector: bfloat16 [8192, 1024], P('dp', 'mp'), may hold values from -0.0625 to 0.0625
- value_projector: bfloat16 [8192, 1024], P('dp', 'mp'), may hold values from -0.0625 to 0.0625
- out_weight: bfloat16 [8192, 8192], P('mp', 'dp'), may hold values from -0.1875 to 0.1875
- key_cache: bfloat16 [8, 8, 256, 128], P(('groups', 'dp'), 'mp'), parts along dimension 0, may hold values from -1230 to 1230
- earlier_value_cache: bfloat16 [8, 8, 256, 128], P(('groups', 'dp'), 'mp'), parts along dimension 0, may hold values from -6 to 6
- cached_length_per_row: int32 [8], P(('groups', 'dp')), parts along dimension 0, may hold values from 1 to 256
- final_gain: float32 [8192], replicated, may hold values from 0.25 to 1.75
- head_weight: bfloat16 [32000, 8192], P('dp', 'mp'), may hold values from -41 to 41
- draft_ids: int32 [8], P(('groups', 'mp')), parts along dimension 0, may hold values from 0 to 31999
Outputs:
- residual_out: bfloat16 [8, 8192], P(('groups', 'mp'), 'dp'), parts along dimension 0
- draft_logprob: float32 [8], P(('groups', 'mp')), parts along dimension 0
There are 2 independent parts, one for each index of `groups`. A program takes and returns all parts, laid end to end along the dimension named above; an argument that names none is the same for every part. Nothing has to cross between parts.
All inputs are finite; a program needn't handle non-finite values.
Results may differ from a plain program's by a relative error of at most 0.0035.
Values may be sent and summed in bfloat16 or wider, within the bound.
A program may use at most 128 MiB of HBM per device.

v0:
```python
import jax
import jax.numpy as jnp
from jax import lax
from jax.sharding import PartitionSpec as P

MODEL_WIDTH = 8192


EPSILON = 1e-05
THETA = 10000.0


def rotary_embedding(vectors, positions):
    half_dim = vectors.shape[-1] // 2
    frequency = THETA ** (-2.0 * jnp.arange(half_dim, dtype=jnp.float32) / vectors.shape[-1])
    angles = positions.astype(jnp.float32)[:, None, None] * frequency[None, None, :]
    cosine = jnp.cos(angles)
    sine_part = jnp.sin(angles)
    former = vectors[..., :half_dim]
    latter = vectors[..., half_dim:]
    return jnp.concatenate(
        [former * cosine - latter * sine_part, latter * cosine + former * sine_part], axis=-1
    )


def rms_normed(matrix, gain_row):
    wide_rows = matrix.astype(jnp.float32)
    mean_square = jnp.mean(wide_rows * wide_rows, axis=-1, keepdims=True)
    return (wide_rows * lax.rsqrt(mean_square + EPSILON) * gain_row).astype(jnp.bfloat16)


def shards(
    hidden,
    attention_gain,
    query_weight,
    key_projector,
    value_projector,
    out_weight,
    key_cache,
    earlier_value_cache,
    cached_length_per_row,
    final_gain,
    head_weight,
    draft_ids,
):
    sequences = key_cache.shape[0]
    local_pairs = key_cache.shape[1]
    head_size = key_cache.shape[3]
    query_cols = query_weight.shape[1]
    pair_cols = key_projector.shape[1]
    local_heads = query_cols // head_size
    group_size = local_heads // local_pairs
    hidden_wide = hidden.astype(jnp.float32)
    squares_in = lax.psum(jnp.sum(hidden_wide * hidden_wide, axis=1), "dp")
    normed = (
        hidden_wide * lax.rsqrt(squares_in / MODEL_WIDTH + EPSILON)[:, None] * attention_gain
    ).astype(jnp.bfloat16)
    all_rows = lax.all_gather(normed, "mp", axis=0, tiled=True)
    picked_rows = all_rows
    projected = lax.psum_scatter(
        jnp.concatenate(
            [
                jnp.dot(picked_rows, weight, preferred_element_type=jnp.float32)
                for weight in (query_weight, key_projector, value_projector)
            ],
            axis=1,
        ),
        "dp",
        scatter_dimension=0,
        tiled=True,
    )
    query_rows = rotary_embedding(
        projected[:, :query_cols].reshape(sequences, local_heads, head_size), cached_length_per_row
    ).astype(jnp.bfloat16)
    query_rows = query_rows.reshape(sequences, local_pairs, group_size, head_size)
    incoming_key = rotary_embedding(
        projected[:, query_cols : query_cols + pair_cols].reshape(
            sequences, local_pairs, head_size
        ),
        cached_length_per_row,
    ).astype(jnp.bfloat16)
    incoming_value = (
        projected[:, query_cols + pair_cols :]
        .reshape(sequences, local_pairs, head_size)
        .astype(jnp.bfloat16)
    )
    score_scale = head_size ** (-0.5)
    own_score = (
        jnp.einsum("bgrd,bgd->bgr", query_rows, incoming_key, preferred_element_type=jnp.float32)
        * score_scale
    )
    scores = (
        jnp.einsum("bgrd,bgtd->bgrt", query_rows, key_cache, preferred_element_type=jnp.float32)
        * score_scale
    )
    places = lax.broadcasted_iota(jnp.int32, scores.shape, 3)
    scores = jnp.where(places < cached_length_per_row[:, None, None, None], scores, -jnp.inf)
    highest = jnp.maximum(jnp.max(scores, axis=3), own_score)
    exponent = jnp.exp(scores - highest[..., None])
    denominator = jnp.sum(exponent, axis=3)
    numerator = jnp.einsum(
        "bgrt,bgtd->bgrd",
        exponent.astype(jnp.bfloat16),
        earlier_value_cache,
        preferred_element_type=jnp.float32,
    )
    own_exp = jnp.exp(own_score - highest)
    denominator = denominator + own_exp
    own_weight = lax.optimization_barrier(own_exp.astype(jnp.bfloat16)).astype(jnp.float32)
    numerator = (
        numerator + own_weight[..., None] * incoming_value.astype(jnp.float32)[:, :, None, :]
    )
    mixed_heads = (
        (numerator / denominator[..., None]).astype(jnp.bfloat16).reshape(sequences, query_cols)
    )
    gathered = lax.all_gather(mixed_heads, "dp", axis=0, tiled=True)
    picked_rows = gathered
    attention_out = lax.psum_scatter(
        jnp.dot(picked_rows, out_weight, preferred_element_type=jnp.float32),
        "mp",
        scatter_dimension=0,
        tiled=True,
    )
    residual_out = (hidden_wide + attention_out).astype(jnp.bfloat16)
    full_rows = lax.all_gather(residual_out, "dp", axis=1, tiled=True)
    full_rows = rms_normed(full_rows, final_gain)
    columns = lax.all_to_all(full_rows, "mp", split_axis=1, concat_axis=0, tiled=True)
    picked_rows = columns
    logits = lax.psum_scatter(
        jnp.einsum("bd,vd->bv", picked_rows, head_weight, preferred_element_type=jnp.float32),
        "mp",
        scatter_dimension=0,
        tiled=True,
    )
    vocab_first = lax.axis_index("dp") * head_weight.shape[0]
    local_peak = jnp.max(logits, axis=1)
    local_mass = jnp.sum(jnp.exp(logits - local_peak[:, None]), axis=1)
    matches = lax.broadcasted_iota(jnp.int32, logits.shape, 1) + vocab_first == draft_ids[:, None]
    target_logit = jnp.sum(jnp.where(matches, logits, 0.0), axis=1)
    overall_peak = lax.pmax(local_peak, "dp")
    total_mass, total_target = lax.psum(
        (local_mass * jnp.exp(local_peak - overall_peak), target_logit), "dp"
    )
    log_total = overall_peak + jnp.log(total_mass)
    return (residual_out, total_target - log_total)


def solution(mesh):
    in_specs = (
        P(("groups", "mp"), "dp"),
        P("dp"),
        P("dp", "mp"),
        P("dp", "mp"),
        P("dp", "mp"),
        P("mp", "dp"),
        P(("groups", "dp"), "mp", None, None),
        P(("groups", "dp"), "mp", None, None),
        P(("groups", "dp")),
        P(),
        P("dp", "mp"),
        P(("groups", "mp")),
    )
    out_specs = (P(("groups", "mp"), "dp"), P(("groups", "mp")))
    return jax.shard_map(shards, mesh=mesh, in_specs=in_specs, out_specs=out_specs, check_vma=False)
```

profile of v0, /device:TPU:0, one launch (start us, length us, event | category | flops | bytes accessed | tf_op | source)
XLA Modules:
  0.0 190.5 jit_solution(16684031391719572066)
XLA Ops:
  7.2 1.4 multiply_reduce_fusion.1
  8.6 14.1 %psum.21 = f32[1]{0:T(128)} all-reduce(f32[1]{0:T(128)} %bitcast.1), channel_id=1, replica_groups=mesh['groups'=2,'dp'=4,'mp'=4] {'dp'}, use_global_device_ids=true, to_apply=%region_1.0 | all-reduce | flops 1 | bytes 8 | tf_op jit(solution)/shard_map/psum | solution.py:54
  23.4 0.7 convert_bitcast_fusion
  24.1 5.2 %all-gather = bf16[4,1,2048]{2,1,0:T(2,128)(2,1)S(1)} all-gather(bf16[1,1,2048]{2,1,0:T(2,128)(2,1)S(1)} %convert_bitcast_fusion), channel_id=1, replica_groups=mesh['groups'=2,'dp'=4,'mp'=4] {'mp'}, dimensions={0}, use_global_device_ids=true | all-gather | bytes 20480 | tf_op jit(solution)/shard_map/all_gather | solution.py:58
  29.3 4.7 %fusion.16 = f32[4,2048]{1,0:T(4,128)S(1)} fusion(bf16[2048,2048]{1,0:T(8,128)(2,1)} %param.14, bf16[4,1,2048]{2,1,0:T(2,128)(2,1)S(1)} %all-gather), kind=kOutput, calls=%fused_computation.23 | convolution fusion | flops 33554432 | bytes 8437760 | tf_op jit(solution)/shard_map/dot_general | solution.py:63
  34.6 16.2 %all-reduce = f32[4,2560]{1,0:T(4,128)S(1)} all-reduce(f32[4,2560]{1,0:T(4,128)S(1)} %pad_maximum_fusion), channel_id=2, replica_groups=mesh['groups'=2,'dp'=4,'mp'=4] {'dp'}, use_global_device_ids=true, to_apply=%region_2.0.clone | all-reduce | flops 10240 | bytes 81920
  51.4 0.7 constant_dynamic-slice_fusion
  52.1 0.7 dynamic-slice.7
  54.4 0.7 fusion.25
  55.3 13.1 %all-gather.1 = bf16[4,1,2048]{2,1,0:T(2,128)(2,1)S(1)} all-gather(bf16[1,1,2048]{2,1,0:T(2,128)(2,1)S(1)} %reshape.192), channel_id=1, replica_groups=mesh['groups'=2,'dp'=4,'mp'=4] {'dp'}, dimensions={0}, use_global_device_ids=true | all-gather | bytes 20480 | tf_op jit(solution)/shard_map/all_gather | solution.py:116
  68.5 4.6 %fusion.9 = f32[4,2048]{1,0:T(4,128)S(1)} fusion(bf16[2048,2048]{1,0:T(8,128)(2,1)} %param.17, bf16[4,1,2048]{2,1,0:T(2,128)(2,1)S(1)} %all-gather.1), kind=kOutput, calls=%fused_computation.16 | convolution fusion | flops 33554432 | bytes 8437760 | tf_op jit(solution)/shard_map/dot_general | solution.py:119
  73.0 10.3 %all-reduce.1 = f32[4,2048]{1,0:T(4,128)S(1)} all-reduce(f32[4,2048]{1,0:T(4,128)S(1)} %fusion.9), channel_id=3, replica_groups=mesh['groups'=2,'dp'=4,'mp'=4] {'mp'}, use_global_device_ids=true, to_apply=%region_5.6.clone | all-reduce | flops 8192 | bytes 65536
  83.9 0.7 fusion.21
  84.6 13.1 %all_gather.11 = bf16[1,8192]{1,0:T(2,128)(2,1)S(1)} all-gather(bf16[1,2048]{1,0:T(2,128)(2,1)S(1)} %fusion.21), channel_id=1, replica_groups=mesh['groups'=2,'dp'=4,'mp'=4] {'dp'}, dimensions={1}, use_global_device_ids=true | all-gather | bytes 20480 | tf_op jit(solution)/shard_map/all_gather | solution.py:125
  97.7 0.7 multiply_reduce_fusion
  99.3 0.6 broadcast.94
  99.9 0.8 reduce.9
  100.7 6.6 %all_to_all.16 = bf16[4,2,1024]{2,1,0:T(2,128)(2,1)S(1)} all-to-all(bf16[4,2,1024]{2,1,0:T(2,128)(2,1)S(1)} %reshape.200), channel_id=1, replica_groups=mesh['groups'=2,'dp'=4,'mp'=4] {'mp'}, dimensions={0} | all-to-all | bytes 32768 | tf_op jit(solution)/shard_map/all_to_all | solution.py:127
  107.3 14.4 %fusion.6 = f32[4,8000]{1,0:T(4,128)} fusion(bf16[8000,2048]{1,0:T(8,128)(2,1)} %param.22, bf16[1,4,2048]{2,0,1:T(2,128)(2,1)S(1)} %bitcast.66), kind=kOutput, calls=%fused_computation.13 | convolution fusion | flops 131072000 | bytes 32912384 | tf_op jit(solution)/shard_map/bd,vd->bv/dot_general | solution.py:130
  122.3 29.9 %all-reduce.6.cloned.1.call-done = f32[4,8000]{1,0:T(4,128)} async-done(((f32[4,8000]{1,0:T(4,128)}), f32[4,8000]{1,0:T(4,128)}) %all-reduce.6.cloned.1.call-update) | async-done | bytes 128016
  152.2 2.3 %dynamic-slice_reduce_fusion = f32[]{:T(128)} fusion(f32[4,8000]{1,0:T(4,128)} %all-reduce.6.cloned.1.call-done, u32[]{:T(128)} %bitcast.28), kind=kLoop, calls=%fused_computation.39 | loop fusion | flops 7999 | bytes 32008 | tf_op jit(solution)/shard_map/reduce_max | solution.py:136
  154.5 12.3 %pmax.7 = f32[1]{0:T(128)} all-reduce(f32[1]{0:T(128)} %bitcast.24), channel_id=1, replica_groups=mesh['groups'=2,'dp'=4,'mp'=4] {'dp'}, use_global_device_ids=true, to_apply=%region_11.12 | all-reduce | flops 1 | bytes 8 | tf_op jit(solution)/shard_map/pmax | solution.py:140
  168.0 3.0 %exponential_reduce_fusion = (f32[]{:T(128)}, f32[]{:T(128)}) fusion(f32[]{:T(128)} %dynamic-slice_reduce_fusion, f32[4,8000]{1,0:T(4,128)} %all-reduce.6.cloned.1.call-done, u32[]{:T(128)} %bitcast.28, s32[]{:T(128)} %bitcast.64, s32[]{:T(128)S(6)} %mul.175), kind=kLoop, calls=%fused_computation.11 | loop fusion | flops 47998 | bytes 32024 | tf_op jit(solution)/shard_map/reduce_sum | solution.py:137
  171.7 8.9 %all-reduce.3 = (f32[1]{0:T(128)}, f32[1]{0:T(128)}) all-reduce(f32[1]{0:T(128)} %bitcast.23, f32[1]{0:T(128)S(6)} %mul.180), channel_id=1, replica_groups=mesh['groups'=2,'dp'=4,'mp'=4] {'dp'}, use_global_device_ids=true, to_apply=%region_9.10 | all-reduce | flops 2 | bytes 16 | tf_op jit(solution)/shard_map/psum | solution.py:141
  (40 shorter events, 3.0 us)
Async XLA Ops:
  7.2 26.9 %copy-start = (bf16[2048,256]{1,0:T(8,128)(2,1)S(1)}, bf16[2048,256]{1,0:T(8,128)(2,1)}, u32[]{:S(2)}) copy-start(bf16[2048,256]{1,0:T(8,128)(2,1)} %param.16) | copy-start | bytes 3145732
  7.2 145.0 %all-reduce.6.cloned.1.call-start = ((), (), s32[]{:S(2)}) async-start(), calls=%async_computation.1 | async-start | bytes 258048
  29.3 4.9 %copy-start.1 = (bf16[2048,256]{1,0:T(8,128)(2,1)S(1)}, bf16[2048,256]{1,0:T(8,128)(2,1)}, u32[]{:S(2)}) copy-start(bf16[2048,256]{1,0:T(8,128)(2,1)} %param.15) | copy-start | bytes 3145732
  29.3 21.5 %copy-start.8 = (u32[32]{0:T(128)S(1)}, u32[32]{0:T(128)}, u32[]{:S(2)}) copy-start(u32[32]{0:T(128)} %constant.41) | copy-start | bytes 388
  29.3 24.6 %copy-start.2 = (bf16[1,2,256,128]{3,2,1,0:T(8,128)(2,1)S(1)}, bf16[1,2,256,128]{3,2,1,0:T(8,128)(2,1)}, u32[]{:S(2)}) copy-start(bf16[1,2,256,128]{3,2,1,0:T(8,128)(2,1)} %param.18) | copy-start | bytes 393220
  29.3 25.8 %copy-start.6 = (bf16[1,2,256,128]{3,2,1,0:T(8,128)(2,1)S(1)}, bf16[1,2,256,128]{3,2,1,0:T(8,128)(2,1)}, u32[]{:S(2)}) copy-start(bf16[1,2,256,128]{3,2,1,0:T(8,128)(2,1)} %param.19) | copy-start | bytes 393220
  34.5 48.8 %copy-start.7 = (u32[32]{0:T(128)S(1)}, u32[32]{0:T(128)}, u32[]{:S(2)}) copy-start(u32[32]{0:T(128)} %constant.45) | copy-start | bytes 388
  34.5 49.4 %copy-start.3 = (bf16[1,2048]{1,0:T(2,128)(2,1)S(1)}, bf16[1,2048]{1,0:T(2,128)(2,1)}, u32[]{:S(2)}) copy-start(bf16[1,2048]{1,0:T(2,128)(2,1)} %param.12) | copy-start | bytes 12292
  34.5 64.7 %copy-start.4 = (f32[8192]{0:T(1024)S(1)}, f32[8192]{0:T(1024)}, u32[]{:S(2)}) copy-start(f32[8192]{0:T(1024)} %param.21) | copy-start | bytes 98308
  84.6 37.0 %copy-start.5 = (bf16[1,2048]{1,0:T(2,128)(2,1)}, bf16[1,2048]{1,0:T(2,128)(2,1)S(1)}, u32[]{:S(2)}) copy-start(bf16[1,2048]{1,0:T(2,128)(2,1)S(1)} %fusion.21) | copy-start | bytes 12292
Sparse Core Ops, SparseCore 0:
  121.8 30.3 all-reduce.5
where the time goes:
time: 191 us
  blocking collectives  99.8 us (52%)
  waiting for transfers between devices  29.9 us (16%)
  matrix products  24.8 us (13%)
  between operations  21.9 us (11%)
  other arithmetic  10.9 us (6%)
  local copies, waits for them, and re-layouts  3.24 us (2%)
    unnamed x2, waiting for transfers between devices  29.9 us
    unnamed x2, blocking collectives  26.5 us
    dot_general x1, matrix products, shards(): jnp.einsum('bd,vd->bv', picked_rows, head_weight, preferred_element_type=...  14.4 us
    psum x1, blocking collectives, shards(): squares_in = lax.psum(jnp.sum(hidden_wide * hidden_wide, axis=1), 'dp')  14.1 us
    all_gather x1, blocking collectives, shards(): full_rows = lax.all_gather(residual_out, 'dp', axis=1, tiled=True)  13.1 us
    all_gather x1, blocking collectives, shards(): gathered = lax.all_gather(mixed_heads, 'dp', axis=0, tiled=True)  13.1 us
    pmax x1, blocking collectives, shards(): overall_peak = lax.pmax(local_peak, 'dp')  12.3 us
    psum x1, blocking collectives, shards(): lax.psum((local_mass * jnp.exp(local_peak - overall_peak), target_logit),...  8.95 us
  transfers between devices with their start and end apart: 1, of which 1 were waited for; matrix products, arithmetic and copies ran while one was open for 0% of the time, Pallas kernels for 0%

commit v1 on v0

v1 whole, which is shorter than its diff:
```python
import functools
import math

import jax
import jax.numpy as jnp
from jax import lax
from jax.experimental import pallas as pl
from jax.experimental.pallas import tpu as pltpu
from jax.sharding import PartitionSpec as P

EPSILON = 1e-05
THETA = 10000.0
LANES = 128
MESH = pl.DeviceIdType.MESH
F32 = jnp.float32
BF16 = jnp.bfloat16


def each(first, last, body):
    if last - first <= 16:
        for k in range(first, last):
            body(k)
    else:

        @pl.loop(first, last)
        def _(k):
            body(k)


def aligned(start):
    return start if isinstance(start, int) else pl.multiple_of(start, LANES)


def kernel(
    n_dp, n_mp, chunk,
    hidden, attention_gain, query_weight, key_projector, value_projector, out_weight,
    key_cache, value_cache, lengths, final_gain, head_weight, draft_ids,
    residual_out, logprob_out,
    hid_v, gain_v, wq_v, wk_v, wv_v, wo_v, kc_v, vc_v, fgain_v, head_v,
    x_recv, x_v, ss_send, ss_recv, proj_send, proj_recv, mix_send, mix_recv, mix_v,
    att_send, att_recv, res_send, res_recv, ss2_send, ss2_recv, y_v,
    log_send, log_recv, fin_send, fin_recv,
    load_sem, head_sem, out_sem,
    x_ss, x_rs, ss_ss, ss_rs, proj_ss, proj_rs, mix_ss, mix_rs, att_ss, att_rs,
    res_ss, res_rs, ss2_ss, ss2_rs, log_ss, log_rs, fin_ss, fin_rs,
):
    j = lax.axis_index("dp")
    i = lax.axis_index("mp")
    count = n_dp * n_mp
    me = j * n_mp + i
    rows, width = hid_v.shape
    total_rows = rows * n_mp
    model_width = width * n_dp
    sequences, pairs, slots, head_size = kc_v.shape
    query_cols = wq_v.shape[1]
    pair_cols = wk_v.shape[1]
    group = query_cols // pair_cols
    quarter = y_v.shape[1]
    blocks = quarter // width
    vocab = head_v.shape[0]
    chunks = log_send.shape[0]
    full = vocab // chunk

    def load(source, target, slot):
        copy = pltpu.make_async_copy(source, target, load_sem.at[slot])
        copy.start()
        return copy

    hid_in = load(hidden, hid_v, 0)
    gain_in = load(attention_gain, gain_v, 1)
    wk_in = load(key_projector, wk_v, 2)
    wv_in = load(value_projector, wv_v, 3)
    wq_in = load(query_weight, wq_v, 4)
    kc_in = load(key_cache, kc_v, 5)
    vc_in = load(value_cache, vc_v, 6)
    wo_in = load(out_weight, wo_v, 7)
    fgain_in = load(final_gain.at[:, pl.ds(pl.multiple_of(i * quarter, LANES), quarter)], fgain_v, 8)

    def head_copy(c):
        size = chunk if c < full else vocab - full * chunk
        return pltpu.make_async_copy(
            head_weight.at[pl.ds(c * chunk, size)], head_v.at[pl.ds(c * chunk, size)], head_sem.at[c]
        )

    for c in range(chunks):
        head_copy(c).start()

    def place(number):
        return {"dp": number // n_mp, "mp": lax.rem(number, n_mp)}

    barrier = pltpu.get_barrier_semaphore()

    def greet(k):
        pl.semaphore_signal(
            barrier, inc=1, device_id=place(lax.rem(me + k, count)), device_id_type=MESH
        )

    each(1, count, greet)

    def remote(source, target, send, receive, device):
        return pltpu.make_async_remote_copy(
            src_ref=source, dst_ref=target, send_sem=send, recv_sem=receive,
            device_id=device, device_id_type=MESH,
        )

    hid_in.wait()
    own = hid_v[...].astype(F32)
    ss_send[...] = jnp.broadcast_to(jnp.sum(own * own, axis=1, keepdims=True), ss_send.shape)
    ss_recv[me] = ss_send[...]
    x_recv[i] = hid_v[...]

    lane = lax.broadcasted_iota(jnp.int32, (1, head_size), 1)
    half = head_size // 2
    index = jnp.where(lane < half, lane, lane - half).astype(F32)
    frequency = jnp.exp(index * (-2.0 * math.log(THETA) / head_size))
    turns = []
    for s in range(sequences):
        angles = lengths[s].astype(F32) * frequency
        sine = jnp.sin(angles)
        turns.append((jnp.cos(angles), jnp.where(lane < half, -sine, sine)))

    pl.semaphore_wait(barrier, count - 1)

    def x_copy(k):
        return remote(
            hid_v, x_recv.at[i], x_ss.at[k], x_rs.at[i], {"dp": j, "mp": lax.rem(i + k, n_mp)}
        )

    def ss_copy(k):
        return remote(
            ss_send, ss_recv.at[me], ss_ss.at[k], ss_rs.at[me], place(lax.rem(me + k, count))
        )

    each(1, count, lambda k: ss_copy(k).start())
    each(1, n_mp, lambda k: x_copy(k).start())

    def arrived(n, mine, buffer, sems):
        def one(k):
            source = lax.rem(mine + k, n)
            pltpu.make_async_copy(buffer.at[source], buffer.at[source], sems.at[source]).wait()

        each(1, n, one)

    def row_scales(buffer):
        scales = []
        for r in range(n_mp):
            squares = buffer[r]
            for d in range(1, n_dp):
                squares += buffer[d * n_mp + r]
            scales.append(lax.rsqrt(squares[:, :1] / model_width + EPSILON))
        return scales

    gain_in.wait()
    arrived(n_mp, i, x_recv, x_rs)
    arrived(count, me, ss_recv, ss_rs)
    scales = row_scales(ss_recv)
    gain = gain_v[...]
    x_v[...] = jnp.concatenate(
        [x_recv[r].astype(F32) * scales[r] * gain for r in range(n_mp)], axis=0
    ).astype(BF16)

    def project(left, weight, keep, base, parts, size):
        columns = weight.shape[1]
        step = min(512, columns)

        def one(c):
            start = aligned(c * step)
            part = jnp.dot(left[...], weight[:, pl.ds(start, step)], preferred_element_type=F32)
            for t in range(parts):
                keep[t, :, pl.ds(aligned(base + start), step)] = part[t * size : (t + 1) * size]

        if columns == step:
            one(0)
        else:

            @pl.loop(0, columns // step)
            def _(c):
                one(c)

    wk_in.wait()
    project(x_v, wk_v, proj_send, query_cols, n_dp, sequences)
    wv_in.wait()
    project(x_v, wv_v, proj_send, query_cols + pair_cols, n_dp, sequences)
    wq_in.wait()
    project(x_v, wq_v, proj_send, 0, n_dp, sequences)

    def proj_copy(k):
        t = lax.rem(j + k, n_dp)
        return remote(
            proj_send.at[t], proj_recv.at[j], proj_ss.at[k], proj_rs.at[j], {"dp": t, "mp": i}
        )

    each(1, n_dp, lambda k: proj_copy(k).start())
    kc_in.wait()
    vc_in.wait()
    arrived(n_dp, j, proj_recv, proj_rs)
    proj_recv[j] = proj_send[j]
    projected = proj_recv[0]
    for d in range(1, n_dp):
        projected += proj_recv[d]

    def rotated(vectors, turn):
        swapped = jnp.concatenate([vectors[:, half:], vectors[:, :half]], axis=1)
        return (vectors * turn[0] + swapped * turn[1]).astype(BF16)

    scale = head_size ** (-0.5)
    for s in range(sequences):
        def heads_of(start, number):
            return jnp.concatenate(
                [
                    projected[s : s + 1, start + h * head_size : start + (h + 1) * head_size]
                    for h in range(number)
                ],
                axis=0,
            )

        queries = rotated(heads_of(0, pairs * group), turns[s])
        keys = rotated(heads_of(query_cols, pairs), turns[s])
        values = heads_of(query_cols + pair_cols, pairs).astype(BF16)
        mixed = []
        for g in range(pairs):
            query = queries[g * group : (g + 1) * group]
            own_score = scale * jnp.sum(
                query.astype(F32) * keys[g : g + 1].astype(F32), axis=1, keepdims=True
            )
            scores = scale * lax.dot_general(
                query, kc_v[s, g], (((1,), (1,)), ((), ())), preferred_element_type=F32
            )
            spots = lax.broadcasted_iota(jnp.int32, scores.shape, 1)
            scores = jnp.where(spots < lengths[s], scores, -jnp.inf)
            highest = jnp.maximum(jnp.max(scores, axis=1, keepdims=True), own_score)
            exponent = jnp.exp(scores - highest)
            own_exp = jnp.exp(own_score - highest)
            denominator = jnp.sum(exponent, axis=1, keepdims=True) + own_exp
            numerator = jnp.dot(exponent.astype(BF16), vc_v[s, g], preferred_element_type=F32)
            numerator += own_exp.astype(BF16).astype(F32) * values[g : g + 1].astype(F32)
            mixed.append(numerator / denominator)
        mixed = [m[h : h + 1] for m in mixed for h in range(group)]
        mix_send[s : s + 1] = jnp.concatenate(mixed, axis=1).astype(BF16)

    def mix_copy(k):
        return remote(
            mix_send, mix_recv.at[j], mix_ss.at[k], mix_rs.at[j],
            {"dp": lax.rem(j + k, n_dp), "mp": i},
        )

    each(1, n_dp, lambda k: mix_copy(k).start())
    mix_recv[j] = mix_send[...]
    wo_in.wait()
    arrived(n_dp, j, mix_recv, mix_rs)
    mix_v[...] = jnp.concatenate(
        [mix_recv[d].astype(F32) for d in range(n_dp)], axis=0
    ).astype(BF16)
    project(mix_v, wo_v, att_send, 0, n_mp, rows)

    def att_copy(k):
        t = lax.rem(i + k, n_mp)
        return remote(
            att_send.at[t], att_recv.at[i], att_ss.at[k], att_rs.at[i], {"dp": j, "mp": t}
        )

    each(1, n_mp, lambda k: att_copy(k).start())
    att_recv[i] = att_send[i]
    arrived(n_mp, i, att_recv, att_rs)
    attended = att_recv[0]
    for r in range(1, n_mp):
        attended += att_recv[r]
    residual = (hid_v[...].astype(F32) + attended).astype(BF16)
    res_send[...] = residual
    wide = residual.astype(F32)
    ss2_send[...] = jnp.broadcast_to(jnp.sum(wide * wide, axis=1, keepdims=True), ss2_send.shape)

    reader = j // blocks
    spot = lax.rem(j, blocks) * n_mp + i

    def res_copy(k):
        return remote(
            res_send, res_recv.at[spot], res_ss.at[k], res_rs.at[spot],
            {"dp": lax.rem(j + k, n_dp), "mp": reader},
        )

    def ss2_copy(k):
        return remote(
            ss2_send, ss2_recv.at[me], ss2_ss.at[k], ss2_rs.at[me], place(lax.rem(me + k, count))
        )

    each(1, n_dp, lambda k: res_copy(k).start())

    @pl.when(reader != i)
    def _():
        res_copy(0).start()

    @pl.when(reader == i)
    def _():
        res_recv[spot] = residual

    each(1, count, lambda k: ss2_copy(k).start())
    ss2_recv[me] = ss2_send[...]
    result = pltpu.make_async_copy(res_send, residual_out, out_sem)
    result.start()

    def res_wait(k):
        source = (i * blocks + k // n_mp) * n_mp + lax.rem(k, n_mp)

        @pl.when(source != me)
        def _():
            pltpu.make_async_copy(res_recv.at[k], res_recv.at[k], res_rs.at[k]).wait()

    each(0, blocks * n_mp, res_wait)
    fgain_in.wait()
    arrived(count, me, ss2_recv, ss2_rs)
    scales = row_scales(ss2_recv)
    y_v[...] = jnp.concatenate(
        [
            jnp.concatenate([res_recv[b * n_mp + r].astype(F32) for b in range(blocks)], axis=1)
            * scales[r]
            * fgain_v[...]
            for r in range(n_mp)
        ],
        axis=0,
    ).astype(BF16)

    def log_copy(c, k):
        t = lax.rem(i + k, n_mp)
        return remote(
            log_send.at[c, t], log_recv.at[c, i], log_ss.at[c * n_mp + k], log_rs.at[c * n_mp + i],
            {"dp": j, "mp": t},
        )

    def head_chunk(c, size):
        piece = 256
        for p in range(0, size, piece):
            wide_piece = min(piece, size - p)
            part = lax.dot_general(
                y_v[...], head_v[pl.ds(c * chunk + p, wide_piece)],
                (((1,), (1,)), ((), ())), preferred_element_type=F32,
            )
            for t in range(n_mp):
                log_send[c, t, :, p : p + wide_piece] = part[t * rows : (t + 1) * rows]
        each(1, n_mp, lambda k: log_copy(c, k).start())

    if full:

        @pl.loop(0, full)
        def _(c):
            start = pl.multiple_of(c * chunk, chunk)
            pltpu.make_async_copy(
                head_weight.at[pl.ds(start, chunk)], head_v.at[pl.ds(start, chunk)], head_sem.at[c]
            ).wait()
            head_chunk(c, chunk)

    if chunks > full:
        rest = vocab - full * chunk
        head_copy(full).wait()
        log_send[full, :, :, rest // LANES * LANES :] = jnp.zeros(
            (n_mp, rows, chunk - rest // LANES * LANES), F32
        )
        head_chunk(full, rest)

    ids = jnp.zeros((rows, 1), jnp.int32)
    row_index = lax.broadcasted_iota(jnp.int32, (rows, 1), 0)
    for r in range(rows):
        ids = jnp.where(row_index == r, draft_ids[r], ids)
    column = lax.broadcasted_iota(jnp.int32, (rows, chunk), 1)
    pieces = []
    target = jnp.zeros((rows, chunk), F32)
    for c in range(chunks):
        logits = log_send[c, i]
        for k in range(1, n_mp):
            source = lax.rem(i + k, n_mp)
            pltpu.make_async_copy(
                log_recv.at[c, source], log_recv.at[c, source], log_rs.at[c * n_mp + source]
            ).wait()
            logits += log_recv[c, source]
        if c >= full:
            logits = jnp.where(column < vocab - c * chunk, logits, -jnp.inf)
        target = jnp.where(column + (c * chunk + j * vocab) == ids, logits, target)
        pieces.append(logits)
    if chunks > full:
        inside = ids < (j + 1) * vocab
        target = jnp.where(inside, target, 0.0)
    peak = pieces[0]
    for piece in pieces[1:]:
        peak = jnp.maximum(peak, piece)
    peak = jnp.max(peak, axis=1, keepdims=True)
    mass = jnp.exp(pieces[0] - peak)
    for piece in pieces[1:]:
        mass += jnp.exp(piece - peak)
    mass = jnp.sum(mass, axis=1, keepdims=True)
    target = jnp.sum(target, axis=1, keepdims=True)
    lanes = lax.broadcasted_iota(jnp.int32, (rows, LANES), 1)
    fin_send[...] = jnp.where(lanes == 0, peak, jnp.where(lanes == 1, mass, target))

    def fin_copy(k):
        return remote(
            fin_send, fin_recv.at[j], fin_ss.at[k], fin_rs.at[j],
            {"dp": lax.rem(j + k, n_dp), "mp": i},
        )

    each(1, n_dp, lambda k: fin_copy(k).start())
    fin_recv[j] = fin_send[...]

    each(1, count, lambda k: ss_copy(k).wait_send())
    each(1, n_mp, lambda k: x_copy(k).wait_send())
    each(1, n_dp, lambda k: proj_copy(k).wait_send())
    each(1, n_dp, lambda k: mix_copy(k).wait_send())
    each(1, n_mp, lambda k: att_copy(k).wait_send())
    each(1, n_dp, lambda k: res_copy(k).wait_send())

    @pl.when(reader != i)
    def _():
        res_copy(0).wait_send()

    each(1, count, lambda k: ss2_copy(k).wait_send())
    for c in range(chunks):
        each(1, n_mp, lambda k: log_copy(c, k).wait_send())
    result.wait()
    arrived(n_dp, j, fin_recv, fin_rs)
    each(1, n_dp, lambda k: fin_copy(k).wait_send())

    tiles = [fin_recv[d] for d in range(n_dp)]
    overall = tiles[0][:, 0:1]
    for tile in tiles[1:]:
        overall = jnp.maximum(overall, tile[:, 0:1])
    mass = jnp.zeros_like(overall)
    target = jnp.zeros_like(overall)
    for tile in tiles:
        mass += tile[:, 1:2] * jnp.exp(tile[:, 0:1] - overall)
        target += tile[:, 2:3]
    logprob = target - (overall + jnp.log(mass))
    for r in range(rows):
        logprob_out[r] = logprob[r, 0]


def solution(mesh):
    n_dp, n_mp = mesh.shape["dp"], mesh.shape["mp"]

    def shards(
        hidden, attention_gain, query_weight, key_projector, value_projector, out_weight,
        key_cache, earlier_value_cache, cached_length_per_row, final_gain, head_weight, draft_ids,
    ):
        rows, width = hidden.shape
        sequences = key_cache.shape[0]
        query_cols = query_weight.shape[1]
        wide = query_cols + key_projector.shape[1] + value_projector.shape[1]
        vocab, quarter = head_weight.shape
        count = n_dp * n_mp
        chunk = min(1024, -(-vocab // LANES) * LANES)
        chunks = -(-vocab // chunk)
        blocks = quarter // width
        vmem, dma = pltpu.VMEM, pltpu.SemaphoreType.DMA
        flat = (1, width)
        scratch = [
            vmem(hidden.shape, BF16), vmem(flat, F32),
            *[vmem(w.shape, BF16) for w in (query_weight, key_projector, value_projector, out_weight)],
            vmem(key_cache.shape, BF16), vmem(earlier_value_cache.shape, BF16),
            vmem((1, quarter), F32), vmem(head_weight.shape, BF16),
            vmem((n_mp, rows, width), BF16), vmem((n_mp * rows, width), BF16),
            vmem((rows, LANES), F32), vmem((count, rows, LANES), F32),
            vmem((n_dp, sequences, wide), F32), vmem((n_dp, sequences, wide), F32),
            vmem((sequences, query_cols), BF16), vmem((n_dp, sequences, query_cols), BF16),
            vmem((n_dp * sequences, query_cols), BF16),
            vmem((n_mp, rows, width), F32), vmem((n_mp, rows, width), F32),
            vmem((rows, width), BF16), vmem((blocks * n_mp, rows, width), BF16),
            vmem((rows, LANES), F32), vmem((count, rows, LANES), F32),
            vmem((n_mp * rows, quarter), BF16),
            vmem((chunks, n_mp, rows, chunk), F32), vmem((chunks, n_mp, rows, chunk), F32),
            vmem((rows, LANES), F32), vmem((n_dp, rows, LANES), F32),
            dma((9,)), dma((chunks,)), dma,
            dma((n_mp,)), dma((n_mp,)), dma((count,)), dma((count,)),
            dma((n_dp,)), dma((n_dp,)), dma((n_dp,)), dma((n_dp,)), dma((n_mp,)), dma((n_mp,)),
            dma((n_dp,)), dma((blocks * n_mp,)), dma((count,)), dma((count,)),
            dma((chunks * n_mp,)), dma((chunks * n_mp,)), dma((n_dp,)), dma((n_dp,)),
        ]
        anywhere = pl.BlockSpec(memory_space=pl.ANY)
        scalars = pl.BlockSpec(memory_space=pltpu.SMEM)
        return pl.pallas_call(
            functools.partial(kernel, n_dp, n_mp, chunk),
            out_shape=(
                jax.ShapeDtypeStruct(hidden.shape, BF16),
                jax.ShapeDtypeStruct(draft_ids.shape, F32),
            ),
            in_specs=[anywhere] * 8 + [scalars] + [anywhere] * 2 + [scalars],
            out_specs=(anywhere, scalars),
            scratch_shapes=scratch,
            compiler_params=pltpu.CompilerParams(
                collective_id=0, has_side_effects=True, vmem_limit_bytes=67043328
            ),
        )(
            hidden, attention_gain.reshape(flat), query_weight, key_projector, value_projector,
            out_weight, key_cache, earlier_value_cache, cached_length_per_row,
            final_gain.reshape(1, -1), head_weight, draft_ids,
        )

    in_specs = (
        P(("groups", "mp"), "dp"),
        P("dp"),
        P("dp", "mp"),
        P("dp", "mp"),
        P("dp", "mp"),
        P("mp", "dp"),
        P(("groups", "dp"), "mp", None, None),
        P(("groups", "dp"), "mp", None, None),
        P(("groups", "dp")),
        P(),
        P("dp", "mp"),
        P(("groups", "mp")),
    )
    out_specs = (P(("groups", "mp"), "dp"), P(("groups", "mp")))
    return jax.shard_map(shards, mesh=mesh, in_specs=in_specs, out_specs=out_specs, check_vma=False)
```

time: 191 us -> 51.9 us (0.27)
  blocking collectives: 99.8 us -> 0 us
  Pallas kernels: 0 us -> 46.6 us
  waiting for transfers between devices: 29.9 us -> 0 us
  matrix products: 24.8 us -> 0 us
  between operations: 21.9 us -> 3.7 us
  other arithmetic: 10.9 us -> 0 us
  local copies, waits for them, and re-layouts: 3.24 us -> 1.3 us
    pallas_call x0 -> x1, Pallas kernels: none -> 46.6 us  [shards(): pl.pallas_call(functools.partial(kernel, n_dp, n_mp, chunk), out_shape=(j...]
    all_gather x3 -> x0, blocking collectives: 31.5 us -> none  [the longest x1 13.1 us: shards(): full_rows = lax.all_gather(residual_out, 'dp', axis=1, tiled=True)]
    unnamed x2 -> x0, waiting for transfers between devices: 29.9 us -> none
    unnamed x2 -> x0, blocking collectives: 26.5 us -> none
    dot_general x8 -> x0, matrix products: 24.8 us -> none  [the longest x1 14.4 us: shards(): jnp.einsum('bd,vd->bv', picked_rows, head_weight, preferred_element_type=...]
    psum x2 -> x0, blocking collectives: 23 us -> none  [the longest x1 14.1 us: shards(): squares_in = lax.psum(jnp.sum(hidden_wide * hidden_wide, axis=1), 'dp')]
    pmax x1 -> x0, blocking collectives: 12.3 us -> none  [shards(): overall_peak = lax.pmax(local_peak, 'dp')]
    all_to_all x1 -> x0, blocking collectives: 6.55 us -> none  [shards(): lax.all_to_all(full_rows, 'mp', split_axis=1, concat_axis=0, tiled=True)]
  transfers between devices with their start and end apart: 1 -> 0, of which waited for: 1 -> 0; matrix products, arithmetic and copies ran while one was open for 0% -> 0% of each run, Pallas kernels for 0% -> 0%
where the time goes in v1:
time: 51.9 us; the launch traced here: 51.6 us
  Pallas kernels  46.6 us (90%)
  between operations  3.7 us (7%)
  local copies, waits for them, and re-layouts  1.3 us (3%)
    pallas_call x1, Pallas kernels, shards(): pl.pallas_call(functools.partial(kernel, n_dp, n_mp, chunk), out_shape=(j...  46.6 us
    unnamed x1, local copies, waits for them, and re-layouts  1.3 us

profile of v1, /device:TPU:0, one launch (start us, length us, event | category | flops | bytes accessed | tf_op | source)
XLA Modules:
  0.0 51.6 jit_solution(14738383383451280513)
XLA Ops:
  1.9 46.6 %shard_map.131 = (bf16[1,2048]{1,0:T(2,128)(2,1)}, f32[1]{0:T(128)}) custom-call(bf16[1,2048]{1,0:T(2,128)(2,1)} %hidden.1, f32[1,2048]{1,0:T(1,128)} %bitcast.3, bf16[2048,2048]{1,0:T(8,128)(2,1)} %query_weight.1, bf16[2048,256]{1,0:T(8,128)(2,1)} %key_projector.1, bf16[2048,256]{1,0:T(8,128)(2,1)} %value_projector.1, bf16[2048,2048]{1,0:T(8,128)(2,1)} %out_weight.1, ...), custom_call_target="tpu_custom_call" | custom-call | tf_op jit(solution)/shard_map/pallas_call | solution.py:477
  48.5 1.3 %copy.18 = bf16[1,2048]{1,0:T(2,128)(2,1)} copy(bf16[1,2048]{1,0:T(2,128)(2,1)} %get-tuple-element.4) | data formatting | bytes 8192
